TPU v7x, 32 devices: a whole 2x2x4 slice. The times are simulated.
32 devices in a mesh: tm: 4 (over y, x), lat: 8 (over z, core).
Axes of the slice: x: 2, y: 2, z: 4, core: 2. Of those that a mesh axis runs over, the one named last changes fastest.
Arguments:
- sketch: bfloat16 [256, 3, 64, 1024], P('tm', None, 'lat'), may hold values from -6 to 6
- test_sketch: bfloat16 [256, 3, 64, 1024], P('tm', None, 'lat'), may hold values from -6 to 6
- checkpoints: bfloat16 [16, 3, 64, 1024], P('tm', None, 'lat'), may hold values from -2.5 to 2.5
- checkpoint_step: int32 [4], P('tm'), may hold values from 0 to 3
- station_row: int32 [4, 1024], P('tm', 'lat'), may hold values from 0 to 63, as said below
- station_column: int32 [4, 1024], P('tm', 'lat'), may hold values from 0 to 1023
- station_value: float32 [4, 1024], P('tm', 'lat'), may hold values from -6 to 6
Outputs:
- increment: float32 [4, 3, 64, 1024], P('tm', None, 'lat')
- reduced_adjoint: float32 [4, 64], P('tm')
- total_cost: float32 [], replicated
Inputs may be any that keep to these rules, and one draw needn't show every extreme that they name: `station_row`: in each group's list, entries 128 * j to 128 * (j + 1) - 1 lie in latitude rows 8 * j to 8 * (j + 1) - 1.
All inputs are finite; a program needn't handle non-finite values.
Results may differ from a plain program's by a relative error of at most 0.0003.
Values may be sent and summed in bfloat16 or wider, within the bound.
A program may use at most 128 MiB of HBM per device.

v0:
```python
import functools
import math

import jax
import jax.numpy as jnp
from jax import lax
from jax.experimental import pallas as pl
from jax.experimental.pallas import tpu as pltpu
from jax.sharding import PartitionSpec as P

STEPS = 4
LANES = 128

wave_coef = 0.5
flow_coef = 0.4
coriolis_coef = 0.5
map_scale = 0.5

MESH = pl.DeviceIdType.MESH


def dlon(field):
    count = field.shape[1]
    return pltpu.roll(field, count - 1, 1) - pltpu.roll(field, 1, 1)


def dlat(field):
    count = field.shape[0]
    return pltpu.roll(field, count - 1, 0) - pltpu.roll(field, 1, 0)


def advance(state, coefs):
    height, east, north = state
    depth, east_flow, north_flow, turn, keep = coefs
    half = 0.5 * wave_coef
    dx_east, dy_north = dlon(east), dlat(north)
    dx_height, dy_height = dlon(height), dlat(height)
    new_east = (
        east + turn * north - half * dx_height - (east_flow * dx_east + north_flow * dlat(east))
    )
    new_north = (
        north - turn * east - half * dy_height - (east_flow * dlon(north) + north_flow * dy_north)
    )
    new_height = (
        height - depth * (dx_east + dy_north) - (east_flow * dx_height + north_flow * dy_height)
    )
    return new_height * keep, new_east * keep, new_north * keep


def advance_adjoint(state, coefs):
    height, east, north = state
    depth, east_flow, north_flow, turn, keep = coefs
    half = 0.5 * wave_coef
    deep = depth * height
    new_height = height + dlon(half * east + east_flow * height) + dlat(
        half * north + north_flow * height
    )
    new_east = east - turn * north + dlon(deep + east_flow * east) + dlat(north_flow * east)
    new_north = north + turn * east + dlon(east_flow * north) + dlat(deep + north_flow * north)
    return new_height * keep, new_east * keep, new_north * keep


def kernel(
    groups,
    bands,
    sketch_hbm,
    test_hbm,
    stored,
    chosen,
    station_row,
    station_column,
    station_value,
    increment,
    adjoint,
    total_cost,
    sketch,
    test,
    coef_ext,
    ext,
    forced,
    folded,
    spread,
    base_send,
    base_recv,
    field_send,
    field_recv,
    last_send,
    last_recv,
    message,
    later_in,
    own_in,
    cost_out,
    cost_in,
    cost_group_out,
    cost_group_in,
    load_sem,
    base_ss,
    base_rs,
    field_ss,
    field_rs,
    last_ss,
    last_rs,
    later_ss,
    later_rs,
    own_ss,
    own_rs,
    cost_ss,
    cost_rs,
    cost_group_ss,
    cost_group_rs,
):
    rank, fields, rows, columns = sketch.shape
    halo = STEPS
    group = lax.axis_index("tm")
    band = lax.axis_index("lat")
    total_rows = rows * bands
    observed = station_row.shape[1] * bands
    tiles = columns // LANES

    load_sketch = pltpu.make_async_copy(sketch_hbm, sketch, load_sem.at[0])
    load_test = pltpu.make_async_copy(test_hbm, test, load_sem.at[1])
    load_sketch.start()
    load_test.start()

    barrier = pltpu.get_barrier_semaphore()
    devices = groups * bands
    me = group * bands + band

    def greet(offset, carry):
        other = lax.rem(me + offset, devices)
        pl.semaphore_signal(
            barrier,
            inc=1,
            device_id={"tm": other // bands, "lat": lax.rem(other, bands)},
            device_id_type=MESH,
        )
        return carry

    lax.fori_loop(1, devices, greet, 0)

    def remote(source, target, send_sem, recv_sem, where):
        return pltpu.make_async_remote_copy(
            src_ref=source,
            dst_ref=target,
            send_sem=send_sem,
            recv_sem=recv_sem,
            device_id=where,
            device_id_type=MESH,
        )

    def halo_copies(send, recv, ss, rs):
        down = remote(send.at[0], recv.at[1], ss.at[0], rs.at[1], {"lat": jnp.maximum(band - 1, 0)})
        up = remote(
            send.at[1], recv.at[0], ss.at[1], rs.at[0], {"lat": jnp.minimum(band + 1, bands - 1)}
        )
        return down, up

    def halo_start(send, recv, ss, rs):
        down, up = halo_copies(send, recv, ss, rs)

        @pl.when(band > 0)
        def _():
            down.start()

        @pl.when(band == 0)
        def _():
            recv[0] = jnp.zeros(recv.shape[1:], recv.dtype)

        @pl.when(band < bands - 1)
        def _():
            up.start()

        @pl.when(band == bands - 1)
        def _():
            recv[1] = jnp.zeros(recv.shape[1:], recv.dtype)

    def halo_wait(send, recv, ss, rs):
        down, up = halo_copies(send, recv, ss, rs)

        @pl.when(band > 0)
        def _():
            up.wait_recv()

        @pl.when(band < bands - 1)
        def _():
            down.wait_recv()

    def halo_drain(send, recv, ss, rs):
        down, up = halo_copies(send, recv, ss, rs)

        @pl.when(band > 0)
        def _():
            down.wait_send()

        @pl.when(band < bands - 1)
        def _():
            up.wait_send()

    base_half = stored[chosen[0]]
    base = base_half.astype(jnp.float32)
    base_send[0] = base[:, :halo]
    base_send[1] = base[:, rows - halo :]

    cells = lax.broadcasted_iota(jnp.int32, (columns, station_column.shape[1]), 0)
    at_column = cells == station_column[...]
    local_row = station_row[...] - band * rows
    at_row = (
        lax.broadcasted_iota(jnp.int32, (rows, station_row.shape[1]), 0) == local_row
    )
    one_hot = at_column.astype(jnp.float32)
    by_row = jnp.dot(
        base_half[0],
        one_hot.astype(jnp.bfloat16),
        preferred_element_type=jnp.float32,
    )
    seen = jnp.sum(jnp.where(at_row, by_row, 0.0), axis=0, keepdims=True)
    innovation = seen - station_value[...]
    weight = 1.0 + 2.0 * station_row[...].astype(jnp.float32) / total_rows
    weighted = weight * innovation
    cost = jnp.sum(weighted * innovation, axis=1, keepdims=True) / (2.0 * groups * observed)
    cost_row = jnp.broadcast_to(cost, (1, LANES))
    cost_out[...] = cost_row
    source = jnp.where(at_row, weighted / (2.0 * math.sqrt(observed)), 0.0)
    forced[0] = lax.dot_general(
        source,
        one_hot,
        (((1,), (1,)), ((), ())),
        precision=lax.Precision.HIGHEST,
        preferred_element_type=jnp.float32,
    )
    for field in range(1, fields):
        forced[field] = jnp.zeros((rows, columns), jnp.float32)

    pl.semaphore_wait(barrier, devices - 1)

    halo_start(base_send, base_recv, base_ss, base_rs)

    def cost_copy(offset):
        other = lax.rem(band + offset, bands)
        return remote(
            cost_out, cost_in.at[band], cost_ss.at[offset], cost_rs.at[band], {"lat": other}
        )

    def cost_arrival(offset):
        other = lax.rem(band + offset, bands)
        return remote(
            cost_out, cost_in.at[other], cost_ss.at[offset], cost_rs.at[other], {"lat": other}
        )

    def each(count, first, action):
        def step(index, carry):
            action(index)
            return carry

        lax.fori_loop(first, count, step, 0)

    each(bands, 1, lambda offset: cost_copy(offset).start())
    cost_in[band] = cost_row

    halo_wait(base_send, base_recv, base_ss, base_rs)
    for field in range(fields):
        coef_ext[field, pl.ds(0, halo)] = base_recv[0, field]
        coef_ext[field, pl.ds(halo, rows)] = base[field]
        coef_ext[field, pl.ds(halo + rows, halo)] = base_recv[1, field]
    coef_ext[0] = 0.5 * wave_coef * (1.0 + 0.25 * coef_ext[0])
    coef_ext[1] = 0.5 * flow_coef * 0.4 * coef_ext[1]
    coef_ext[2] = 0.5 * flow_coef * 0.4 * coef_ext[2]
    span = rows + 2 * halo

    def coefs():
        where = band * rows - halo + lax.broadcasted_iota(jnp.int32, (span, columns), 0)
        latitude = where.astype(jnp.float32)
        turn = wave_coef * coriolis_coef * (2.0 * (latitude + 0.5) / total_rows - 1.0)
        keep = jnp.where((where >= 0) & (where < total_rows), 1.0, 0.0)
        return coef_ext[0], coef_ext[1], coef_ext[2], turn, keep

    def marched(step_of, send, recv, ss, rs):
        halo_start(send, recv, ss, rs)
        halo_wait(send, recv, ss, rs)
        for field in range(fields):
            ext[field, pl.ds(0, halo)] = recv[0, field]
            ext[field, pl.ds(halo + rows, halo)] = recv[1, field]

        def one(index, carry):
            result = step_of((ext[0], ext[1], ext[2]), coefs())
            for field in range(fields):
                ext[field] = result[field]
            return carry

        lax.fori_loop(0, STEPS, one, 0)

    eye = lax.broadcasted_iota(jnp.int32, (rank, LANES), 0) == lax.broadcasted_iota(
        jnp.int32, (rank, LANES), 1
    )

    def spread_row(row):
        column = jnp.sum(jnp.where(eye, row, 0.0), axis=1, keepdims=True)
        spread[...] = jnp.broadcast_to(column, (rank, LANES))

    block = 4

    def combined(basis, send):
        for field in range(fields):

            def some(index, total):
                for inner in range(block):
                    k = index * block + inner
                    factor = jnp.broadcast_to(spread[pl.ds(k, 1), :], (rows, LANES))
                    total = total + basis[k, field].astype(jnp.float32) * jnp.concatenate(
                        [factor] * tiles, axis=1
                    )
                return total

            total = lax.fori_loop(
                0, rank // block, some, jnp.zeros((rows, columns), jnp.float32)
            )
            ext[field, pl.ds(halo, rows)] = total
            send[0, field] = total[:halo]
            send[1, field] = total[rows - halo :]

    load_sketch.wait()
    load_test.wait()

    @pl.when(group < groups - 1)
    def _():
        def arrive(offset):
            remote(
                message,
                later_in.at[offset],
                later_ss.at[offset],
                later_rs.at[offset],
                {"tm": group, "lat": offset},
            ).wait_recv()

        each(bands, 0, arrive)
        spread_row(jnp.sum(later_in[...], axis=0))
        combined(test, field_send)
        marched(advance_adjoint, field_send, field_recv, field_ss, field_rs)
        scale = map_scale / math.sqrt(rank * fields * total_rows * columns)
        for field in range(fields):
            forced[field] = forced[field] + scale * ext[field, pl.ds(halo, rows)]

    def fold(index, carry):
        for inner in range(block):
            k = index * block + inner
            product = sketch[k, 0].astype(jnp.float32) * forced[0]
            for field in range(1, fields):
                product = product + sketch[k, field].astype(jnp.float32) * forced[field]
            total = product[:, :LANES]
            for tile in range(1, tiles):
                total = total + product[:, tile * LANES : (tile + 1) * LANES]
            folded[k] = total
        return carry

    lax.fori_loop(0, rank // block, fold, 0)
    share = jnp.sum(jnp.sum(folded[...], axis=1), axis=1, keepdims=True)
    share_row = jnp.sum(jnp.where(eye, share, 0.0), axis=0, keepdims=True)
    message[...] = share_row

    def later_copy(offset):
        other = lax.rem(band + offset, bands)
        return remote(
            message,
            later_in.at[band],
            later_ss.at[offset],
            later_rs.at[band],
            {"tm": jnp.maximum(group - 1, 0), "lat": other},
        )

    @pl.when(group > 0)
    def _():
        each(bands, 0, lambda offset: later_copy(offset).start())

    def own_copy(offset):
        other = lax.rem(band + offset, bands)
        return remote(
            message, own_in.at[band], own_ss.at[offset], own_rs.at[band], {"lat": other}
        )

    def own_arrival(offset):
        other = lax.rem(band + offset, bands)
        return remote(
            message, own_in.at[other], own_ss.at[offset], own_rs.at[other], {"lat": other}
        )

    each(bands, 1, lambda offset: own_copy(offset).start())
    own_in[band] = share_row

    each(bands, 1, lambda offset: cost_arrival(offset).wait_recv())
    group_cost = jnp.sum(cost_in[...], axis=0)
    cost_group_out[...] = group_cost

    def cost_group_copy(offset):
        other = lax.rem(group + offset, groups)
        return remote(
            cost_group_out,
            cost_group_in.at[group],
            cost_group_ss.at[offset],
            cost_group_rs.at[group],
            {"tm": other},
        )

    def cost_group_arrival(offset):
        other = lax.rem(group + offset, groups)
        return remote(
            cost_group_out,
            cost_group_in.at[other],
            cost_group_ss.at[offset],
            cost_group_rs.at[other],
            {"tm": other},
        )

    each(groups, 1, lambda offset: cost_group_copy(offset).start())
    cost_group_in[group] = group_cost

    each(bands, 1, lambda offset: own_arrival(offset).wait_recv())
    adjoint_row = jnp.sum(own_in[...], axis=0)
    adjoint[...] = adjoint_row[:, :rank]
    spread_row(adjoint_row)
    combined(sketch, last_send)
    marched(advance, last_send, last_recv, last_ss, last_rs)
    for field in range(fields):
        increment[0, field] = ext[field, pl.ds(halo, rows)] / math.sqrt(rank)

    each(groups, 1, lambda offset: cost_group_arrival(offset).wait_recv())
    total_cost[...] = jnp.sum(cost_group_in[...], axis=0)[:, :1]

    halo_drain(base_send, base_recv, base_ss, base_rs)
    halo_drain(last_send, last_recv, last_ss, last_rs)
    each(bands, 1, lambda offset: cost_copy(offset).wait_send())
    each(bands, 1, lambda offset: own_copy(offset).wait_send())
    each(groups, 1, lambda offset: cost_group_copy(offset).wait_send())

    @pl.when(group < groups - 1)
    def _():
        halo_drain(field_send, field_recv, field_ss, field_rs)

    @pl.when(group > 0)
    def _():
        each(bands, 0, lambda offset: later_copy(offset).wait_send())


def body(
    groups,
    bands,
    sketch,
    test_sketch,
    checkpoints,
    checkpoint_step,
    station_row,
    station_column,
    station_value,
):
    rank, fields, rows, columns = sketch.shape
    span = rows + 2 * STEPS
    f32 = jnp.float32
    vmem = pl.BlockSpec(memory_space=pltpu.VMEM)
    edge = pltpu.VMEM((2, fields, STEPS, columns), f32)
    dma = pltpu.SemaphoreType.DMA
    increment, adjoint, cost = pl.pallas_call(
        functools.partial(kernel, groups, bands),
        out_shape=(
            jax.ShapeDtypeStruct((1, fields, rows, columns), f32),
            jax.ShapeDtypeStruct((1, rank), f32),
            jax.ShapeDtypeStruct((1, 1), f32),
        ),
        in_specs=[
            pl.BlockSpec(memory_space=pl.ANY),
            pl.BlockSpec(memory_space=pl.ANY),
            vmem,
            pl.BlockSpec(memory_space=pltpu.SMEM),
            vmem,
            vmem,
            vmem,
        ],
        out_specs=(vmem, vmem, vmem),
        scratch_shapes=[
            pltpu.VMEM(sketch.shape, sketch.dtype),
            pltpu.VMEM(test_sketch.shape, test_sketch.dtype),
            pltpu.VMEM((fields, span, columns), f32),
            pltpu.VMEM((fields, span, columns), f32),
            pltpu.VMEM((fields, rows, columns), f32),
            pltpu.VMEM((rank, rows, LANES), f32),
            pltpu.VMEM((rank, LANES), f32),
            edge,
            edge,
            edge,
            edge,
            edge,
            edge,
            pltpu.VMEM((1, LANES), f32),
            pltpu.VMEM((bands, 1, LANES), f32),
            pltpu.VMEM((bands, 1, LANES), f32),
            pltpu.VMEM((1, LANES), f32),
            pltpu.VMEM((bands, 1, LANES), f32),
            pltpu.VMEM((1, LANES), f32),
            pltpu.VMEM((groups, 1, LANES), f32),
            dma((2,)),
            dma((2,)),
            dma((2,)),
            dma((2,)),
            dma((2,)),
            dma((2,)),
            dma((2,)),
            dma((bands,)),
            dma((bands,)),
            dma((bands,)),
            dma((bands,)),
            dma((bands,)),
            dma((bands,)),
            dma((groups,)),
            dma((groups,)),
        ],
        compiler_params=pltpu.CompilerParams(
            collective_id=0,
            has_side_effects=True,
            vmem_limit_bytes=40 * 1024 * 1024,
        ),
    )(
        sketch,
        test_sketch,
        checkpoints,
        checkpoint_step,
        station_row,
        station_column,
        station_value,
    )
    return increment, adjoint, cost[0, 0]


def solution(mesh):
    placed = (
        P("tm", None, "lat", None),
        P("tm", None, "lat", None),
        P("tm", None, "lat", None),
        P("tm"),
        P("tm", "lat"),
        P("tm", "lat"),
        P("tm", "lat"),
    )
    return jax.shard_map(
        functools.partial(body, mesh.shape["tm"], mesh.shape["lat"]),
        mesh=mesh,
        in_specs=placed,
        out_specs=(P("tm", None, "lat", None), P("tm", None), P()),
        check_vma=False,
    )
```

profile of v0, /device:TPU:1, one launch (start us, length us, event | category | flops | bytes accessed | tf_op | source)
XLA Modules:
  0.0 54.7 jit_solution(13178289736713578548)
XLA Ops:
  1.3 0.0 copy-start
  1.3 1.9 %copy-done = bf16[64,3,8,1024]{3,2,1,0:T(8,128)(2,1)S(1)} copy-done((bf16[64,3,8,1024]{3,2,1,0:T(8,128)(2,1)S(1)}, bf16[64,3,8,1024]{3,2,1,0:T(8,128)(2,1)}, u32[]{:S(2)}) %copy-start) | copy-done | bytes 3145752
  3.2 0.0 copy-start.1
  3.2 1.9 %copy-done.1 = bf16[64,3,8,1024]{3,2,1,0:T(8,128)(2,1)S(1)} copy-done((bf16[64,3,8,1024]{3,2,1,0:T(8,128)(2,1)S(1)}, bf16[64,3,8,1024]{3,2,1,0:T(8,128)(2,1)}, u32[]{:S(2)}) %copy-start.1) | copy-done | bytes 3145752
  5.1 0.0 copy-start.2
  5.1 0.9 %copy-done.2 = bf16[4,3,8,1024]{3,2,1,0:T(8,128)(2,1)S(1)} copy-done((bf16[4,3,8,1024]{3,2,1,0:T(8,128)(2,1)S(1)}, bf16[4,3,8,1024]{3,2,1,0:T(8,128)(2,1)}, u32[]{:S(2)}) %copy-start.2) | copy-done | bytes 196632
  6.0 0.0 copy-start.3
  6.0 0.7 %copy-done.3 = s32[1,128]{1,0:T(1,128)S(1)} copy-done((s32[1,128]{1,0:T(1,128)S(1)}, s32[1,128]{1,0:T(1,128)}, u32[]{:S(2)}) %copy-start.3) | copy-done | bytes 536
  6.6 0.0 copy-start.4
  6.6 0.7 %copy-done.4 = s32[1,128]{1,0:T(1,128)S(1)} copy-done((s32[1,128]{1,0:T(1,128)S(1)}, s32[1,128]{1,0:T(1,128)}, u32[]{:S(2)}) %copy-start.4) | copy-done | bytes 536
  7.3 0.0 copy-start.5
  7.3 0.7 %copy-done.5 = f32[1,128]{1,0:T(1,128)S(1)} copy-done((f32[1,128]{1,0:T(1,128)S(1)}, f32[1,128]{1,0:T(1,128)}, u32[]{:S(2)}) %copy-start.5) | copy-done | bytes 536
  8.0 43.8 %shard_map.94 = (f32[1,3,8,1024]{3,2,1,0:T(8,128)S(1)}, f32[1,64]{1,0:T(1,128)S(1)}, f32[1,1]{1,0:T(1,128)}) custom-call(bf16[64,3,8,1024]{3,2,1,0:T(8,128)(2,1)S(1)} %copy-done, bf16[64,3,8,1024]{3,2,1,0:T(8,128)(2,1)S(1)} %copy-done.1, bf16[4,3,8,1024]{3,2,1,0:T(8,128)(2,1)S(1)} %copy-done.2, s32[1]{0:T(128)S(6)} %copy.13.chosen, s32[1,128]{1,0:T(1,128)S(1)} %copy-done.3, ...), custom_call_target="tpu_custom_call" | custom-call | tf_op jit(solution)/shard_map/pallas_call | solution.py:460
  51.7 0.6 %copy.14 = f32[1,3,8,1024]{3,2,1,0:T(8,128)} copy(f32[1,3,8,1024]{3,2,1,0:T(8,128)S(1)} %get-tuple-element.12) | data formatting | bytes 196608
  52.4 0.5 copy.15
Async XLA Ops:
  1.3 1.9 %copy-start = (bf16[64,3,8,1024]{3,2,1,0:T(8,128)(2,1)S(1)}, bf16[64,3,8,1024]{3,2,1,0:T(8,128)(2,1)}, u32[]{:S(2)}) copy-start(bf16[64,3,8,1024]{3,2,1,0:T(8,128)(2,1)} %sketch_hbm.1) | copy-start | bytes 9437188
  3.2 1.9 %copy-start.1 = (bf16[64,3,8,1024]{3,2,1,0:T(8,128)(2,1)S(1)}, bf16[64,3,8,1024]{3,2,1,0:T(8,128)(2,1)}, u32[]{:S(2)}) copy-start(bf16[64,3,8,1024]{3,2,1,0:T(8,128)(2,1)} %test_hbm.1) | copy-start | bytes 9437188
  5.1 0.9 %copy-start.2 = (bf16[4,3,8,1024]{3,2,1,0:T(8,128)(2,1)S(1)}, bf16[4,3,8,1024]{3,2,1,0:T(8,128)(2,1)}, u32[]{:S(2)}) copy-start(bf16[4,3,8,1024]{3,2,1,0:T(8,128)(2,1)} %stored.1) | copy-start | bytes 589828
  6.0 0.7 %copy-start.3 = (s32[1,128]{1,0:T(1,128)S(1)}, s32[1,128]{1,0:T(1,128)}, u32[]{:S(2)}) copy-start(s32[1,128]{1,0:T(1,128)} %station_row.1) | copy-start | bytes 1540
  6.6 0.7 %copy-start.4 = (s32[1,128]{1,0:T(1,128)S(1)}, s32[1,128]{1,0:T(1,128)}, u32[]{:S(2)}) copy-start(s32[1,128]{1,0:T(1,128)} %station_column.1) | copy-start | bytes 1540
  7.3 0.7 %copy-start.5 = (f32[1,128]{1,0:T(1,128)S(1)}, f32[1,128]{1,0:T(1,128)}, u32[]{:S(2)}) copy-start(f32[1,128]{1,0:T(1,128)} %station_value.1) | copy-start | bytes 1540
where the time goes:
time: 55 us; the launch traced here: 54.7 us
  Pallas kernels  43.8 us (80%)
  local copies, waits for them, and re-layouts  7.82 us (14%)
  between operations  3.12 us (6%)
    pallas_call x1, Pallas kernels, body(): pl.pallas_call(functools.partial(kernel, groups, bands), out_shape=(jax.S...  43.8 us
    unnamed x14, local copies, waits for them, and re-layouts  7.82 us

commit v1 on v0

--- a/solution.py
+++ b/solution.py
@@ -65,19 +65,25 @@
     bands,
     sketch_hbm,
     test_hbm,
-    stored,
+    stored_hbm,
     chosen,
-    station_row,
-    station_column,
-    station_value,
+    row_hbm,
+    column_hbm,
+    value_hbm,
     increment,
     adjoint,
     total_cost,
     sketch,
     test,
+    beyond,
+    stored,
+    station_row,
+    station_column,
+    station_value,
     coef_ext,
     ext,
     forced,
+    forced_beyond,
     folded,
     spread,
     base_send,
@@ -94,6 +100,8 @@
     cost_group_out,
     cost_group_in,
     load_sem,
+    beyond_ss,
+    beyond_rs,
     base_ss,
     base_rs,
     field_ss,
@@ -117,10 +125,21 @@
     observed = station_row.shape[1] * bands
     tiles = columns // LANES
 
-    load_sketch = pltpu.make_async_copy(sketch_hbm, sketch, load_sem.at[0])
-    load_test = pltpu.make_async_copy(test_hbm, test, load_sem.at[1])
-    load_sketch.start()
-    load_test.start()
+    loads = [
+        pltpu.make_async_copy(source, target, load_sem.at[index])
+        for index, (source, target) in enumerate(
+            (
+                (row_hbm, station_row),
+                (column_hbm, station_column),
+                (value_hbm, station_value),
+                (stored_hbm, stored),
+                (sketch_hbm, sketch),
+                (test_hbm, test),
+            )
+        )
+    ]
+    for load in loads:
+        load.start()
 
     barrier = pltpu.get_barrier_semaphore()
     devices = groups * bands
@@ -148,15 +167,19 @@
             device_id_type=MESH,
         )
 
-    def halo_copies(send, recv, ss, rs):
-        down = remote(send.at[0], recv.at[1], ss.at[0], rs.at[1], {"lat": jnp.maximum(band - 1, 0)})
-        up = remote(
-            send.at[1], recv.at[0], ss.at[1], rs.at[0], {"lat": jnp.minimum(band + 1, bands - 1)}
-        )
+    below = {"lat": jnp.maximum(band - 1, 0)}
+    above = {"lat": jnp.minimum(band + 1, bands - 1)}
+
+    def halo_copies(send, recv, ss, rs, field):
+        down = remote(
+            send.at[0, field], recv.at[1, field], ss.at[0, field], rs.at[1, field], below
+        )
+        up = remote(send.at[1, field], recv.at[0, field], ss.at[1, field], rs.at[0, field], above)
         return down, up
 
-    def halo_start(send, recv, ss, rs):
-        down, up = halo_copies(send, recv, ss, rs)
+    def halo_start(exchange, field):
+        recv = exchange[1]
+        down, up = halo_copies(*exchange, field)
 
         @pl.when(band > 0)
         def _():
@@ -164,7 +187,7 @@
 
         @pl.when(band == 0)
         def _():
-            recv[0] = jnp.zeros(recv.shape[1:], recv.dtype)
+            recv[0, field] = jnp.zeros(recv.shape[2:], recv.dtype)
 
         @pl.when(band < bands - 1)
         def _():
@@ -172,29 +195,36 @@
 
         @pl.when(band == bands - 1)
         def _():
-            recv[1] = jnp.zeros(recv.shape[1:], recv.dtype)
-
-    def halo_wait(send, recv, ss, rs):
-        down, up = halo_copies(send, recv, ss, rs)
-
+            recv[1, field] = jnp.zeros(recv.shape[2:], recv.dtype)
+
+    def halo_wait(exchange):
         @pl.when(band > 0)
         def _():
-            up.wait_recv()
+            for field in range(fields):
+                halo_copies(*exchange, field)[1].wait_recv()
 
         @pl.when(band < bands - 1)
         def _():
-            down.wait_recv()
-
-    def halo_drain(send, recv, ss, rs):
-        down, up = halo_copies(send, recv, ss, rs)
-
+            for field in range(fields):
+                halo_copies(*exchange, field)[0].wait_recv()
+
+    def halo_drain(exchange):
         @pl.when(band > 0)
         def _():
-            down.wait_send()
+            for field in range(fields):
+                halo_copies(*exchange, field)[0].wait_send()
 
         @pl.when(band < bands - 1)
         def _():
-            up.wait_send()
+            for field in range(fields):
+                halo_copies(*exchange, field)[1].wait_send()
+
+    base_halo = (base_send, base_recv, base_ss, base_rs)
+    field_halo = (field_send, field_recv, field_ss, field_rs)
+    last_halo = (last_send, last_recv, last_ss, last_rs)
+
+    for load in loads[:4]:
+        load.wait()
 
     base_half = stored[chosen[0]]
     base = base_half.astype(jnp.float32)
@@ -231,9 +261,96 @@
     for field in range(1, fields):
         forced[field] = jnp.zeros((rows, columns), jnp.float32)
 
+    eye = lax.broadcasted_iota(jnp.int32, (rank, LANES), 0) == lax.broadcasted_iota(
+        jnp.int32, (rank, LANES), 1
+    )
+
+    def spread_row(row):
+        column = jnp.sum(jnp.where(eye, row, 0.0), axis=1, keepdims=True)
+        spread[...] = jnp.broadcast_to(column, (rank, LANES))
+
+    block = 8
+
+    def combined(basis, field):
+        def some(index, total):
+            for inner in range(block):
+                k = index * block + inner
+                factor = jnp.broadcast_to(spread[pl.ds(k, 1), :], (rows, LANES))
+                total = total + basis[k, field].astype(jnp.float32) * jnp.concatenate(
+                    [factor] * tiles, axis=1
+                )
+            return total
+
+        return lax.fori_loop(0, rank // block, some, jnp.zeros((rows, columns), jnp.float32))
+
+    def fold(pairs):
+        def some(index, carry):
+            for inner in range(block):
+                k = index * block + inner
+                product = None
+                for basis, values in pairs:
+                    for field in range(fields):
+                        term = basis[k, field].astype(jnp.float32) * values[field]
+                        product = term if product is None else product + term
+                total = product[:, :LANES]
+                for tile in range(1, tiles):
+                    total = total + product[:, tile * LANES : (tile + 1) * LANES]
+                folded[k] = total
+            return carry
+
+        lax.fori_loop(0, rank // block, some, 0)
+        share = jnp.sum(jnp.sum(folded[...], axis=1), axis=1, keepdims=True)
+        message[...] = jnp.sum(jnp.where(eye, share, 0.0), axis=0, keepdims=True)
+
+    last_group = groups - 1
+    loads[4].wait()
+
+    @pl.when(group == last_group)
+    def _():
+        fold(((sketch, forced),))
+
     pl.semaphore_wait(barrier, devices - 1)
 
-    halo_start(base_send, base_recv, base_ss, base_rs)
+    for field in range(fields):
+        halo_start(base_halo, field)
+
+    def each(count, first, action):
+        for index in range(first, count):
+            action(index)
+
+    def later_copy(offset):
+        other = lax.rem(band + offset, bands)
+        return remote(
+            message,
+            later_in.at[band],
+            later_ss.at[offset],
+            later_rs.at[band],
+            {"tm": jnp.maximum(group - 1, 0), "lat": other},
+        )
+
+    def own_copy(offset):
+        other = lax.rem(band + offset, bands)
+        return remote(
+            message, own_in.at[band], own_ss.at[offset], own_rs.at[band], {"lat": other}
+        )
+
+    def own_arrival(offset):
+        other = lax.rem(band + offset, bands)
+        return remote(
+            message, own_in.at[other], own_ss.at[offset], own_rs.at[other], {"lat": other}
+        )
+
+    def announce():
+        @pl.when(group > 0)
+        def _():
+            each(bands, 0, lambda offset: later_copy(offset).start())
+
+        each(bands, 1, lambda offset: own_copy(offset).start())
+        own_in[band] = message[...]
+
+    @pl.when(group == last_group)
+    def _():
+        announce()
 
     def cost_copy(offset):
         other = lax.rem(band + offset, bands)
@@ -247,25 +364,57 @@
             cost_out, cost_in.at[other], cost_ss.at[offset], cost_rs.at[other], {"lat": other}
         )
 
-    def each(count, first, action):
-        def step(index, carry):
-            action(index)
-            return carry
-
-        lax.fori_loop(first, count, step, 0)
-
     each(bands, 1, lambda offset: cost_copy(offset).start())
     cost_in[band] = cost_row
 
-    halo_wait(base_send, base_recv, base_ss, base_rs)
+    low, high = pl.ds(0, halo), pl.ds(halo, halo)
+    top = pl.ds(rows - halo, halo)
+    beyond_down = remote(
+        sketch.at[:, :, low], beyond.at[:, :, high], beyond_ss.at[0], beyond_rs.at[1], below
+    )
+    beyond_up = remote(
+        sketch.at[:, :, top], beyond.at[:, :, low], beyond_ss.at[1], beyond_rs.at[0], above
+    )
+
+    def clear(place):
+        def one(k, carry):
+            for field in range(fields):
+                beyond[k, field, place] = jnp.zeros((halo, columns), beyond.dtype)
+            return carry
+
+        lax.fori_loop(0, rank, one, 0)
+
+    @pl.when(group == 0)
+    def _():
+        @pl.when(band > 0)
+        def _():
+            beyond_down.start()
+
+        @pl.when(band == 0)
+        def _():
+            clear(low)
+
+        @pl.when(band < bands - 1)
+        def _():
+            beyond_up.start()
+
+        @pl.when(band == bands - 1)
+        def _():
+            clear(high)
+
+    halo_wait(base_halo)
+    scales = (0.5 * wave_coef * 0.25, 0.5 * flow_coef * 0.4, 0.5 * flow_coef * 0.4)
+    starts = (0.5 * wave_coef, 0.0, 0.0)
     for field in range(fields):
-        coef_ext[field, pl.ds(0, halo)] = base_recv[0, field]
-        coef_ext[field, pl.ds(halo, rows)] = base[field]
-        coef_ext[field, pl.ds(halo + rows, halo)] = base_recv[1, field]
-    coef_ext[0] = 0.5 * wave_coef * (1.0 + 0.25 * coef_ext[0])
-    coef_ext[1] = 0.5 * flow_coef * 0.4 * coef_ext[1]
-    coef_ext[2] = 0.5 * flow_coef * 0.4 * coef_ext[2]
+        for place, part in (
+            (pl.ds(0, halo), base_recv[0, field]),
+            (pl.ds(halo, rows), base[field]),
+            (pl.ds(halo + rows, halo), base_recv[1, field]),
+        ):
+            coef_ext[field, place] = starts[field] + scales[field] * part
     span = rows + 2 * halo
+    inside = pl.ds(halo, rows)
+    before, after = pl.ds(0, halo), pl.ds(halo + rows, halo)
 
     def coefs():
         where = band * rows - halo + lax.broadcasted_iota(jnp.int32, (span, columns), 0)
@@ -274,13 +423,7 @@
         keep = jnp.where((where >= 0) & (where < total_rows), 1.0, 0.0)
         return coef_ext[0], coef_ext[1], coef_ext[2], turn, keep
 
-    def marched(step_of, send, recv, ss, rs):
-        halo_start(send, recv, ss, rs)
-        halo_wait(send, recv, ss, rs)
-        for field in range(fields):
-            ext[field, pl.ds(0, halo)] = recv[0, field]
-            ext[field, pl.ds(halo + rows, halo)] = recv[1, field]
-
+    def march(step_of):
         def one(index, carry):
             result = step_of((ext[0], ext[1], ext[2]), coefs())
             for field in range(fields):
@@ -289,39 +432,28 @@
 
         lax.fori_loop(0, STEPS, one, 0)
 
-    eye = lax.broadcasted_iota(jnp.int32, (rank, LANES), 0) == lax.broadcasted_iota(
-        jnp.int32, (rank, LANES), 1
-    )
-
-    def spread_row(row):
-        column = jnp.sum(jnp.where(eye, row, 0.0), axis=1, keepdims=True)
-        spread[...] = jnp.broadcast_to(column, (rank, LANES))
-
-    block = 4
-
-    def combined(basis, send):
+    def banded(basis, exchange):
+        send, recv = exchange[:2]
         for field in range(fields):
-
-            def some(index, total):
-                for inner in range(block):
-                    k = index * block + inner
-                    factor = jnp.broadcast_to(spread[pl.ds(k, 1), :], (rows, LANES))
-                    total = total + basis[k, field].astype(jnp.float32) * jnp.concatenate(
-                        [factor] * tiles, axis=1
-                    )
-                return total
-
-            total = lax.fori_loop(
-                0, rank // block, some, jnp.zeros((rows, columns), jnp.float32)
-            )
-            ext[field, pl.ds(halo, rows)] = total
+            total = combined(basis, field)
             send[0, field] = total[:halo]
             send[1, field] = total[rows - halo :]
-
-    load_sketch.wait()
-    load_test.wait()
-
-    @pl.when(group < groups - 1)
+            halo_start(exchange, field)
+            ext[field, inside] = total
+        halo_wait(exchange)
+        for field in range(fields):
+            ext[field, before] = recv[0, field]
+            ext[field, after] = recv[1, field]
+
+    map_factor = map_scale / math.sqrt(rank * fields * total_rows * columns)
+
+    def add_mapped():
+        for field in range(fields):
+            forced[field] = forced[field] + map_factor * ext[field, inside]
+
+    loads[5].wait()
+
+    @pl.when(group < last_group)
     def _():
         def arrive(offset):
             remote(
@@ -334,57 +466,37 @@
 
         each(bands, 0, arrive)
         spread_row(jnp.sum(later_in[...], axis=0))
-        combined(test, field_send)
-        marched(advance_adjoint, field_send, field_recv, field_ss, field_rs)
-        scale = map_scale / math.sqrt(rank * fields * total_rows * columns)
-        for field in range(fields):
-            forced[field] = forced[field] + scale * ext[field, pl.ds(halo, rows)]
-
-    def fold(index, carry):
-        for inner in range(block):
-            k = index * block + inner
-            product = sketch[k, 0].astype(jnp.float32) * forced[0]
-            for field in range(1, fields):
-                product = product + sketch[k, field].astype(jnp.float32) * forced[field]
-            total = product[:, :LANES]
-            for tile in range(1, tiles):
-                total = total + product[:, tile * LANES : (tile + 1) * LANES]
-            folded[k] = total
-        return carry
-
-    lax.fori_loop(0, rank // block, fold, 0)
-    share = jnp.sum(jnp.sum(folded[...], axis=1), axis=1, keepdims=True)
-    share_row = jnp.sum(jnp.where(eye, share, 0.0), axis=0, keepdims=True)
-    message[...] = share_row
-
-    def later_copy(offset):
-        other = lax.rem(band + offset, bands)
-        return remote(
-            message,
-            later_in.at[band],
-            later_ss.at[offset],
-            later_rs.at[band],
-            {"tm": jnp.maximum(group - 1, 0), "lat": other},
-        )
-
-    @pl.when(group > 0)
-    def _():
-        each(bands, 0, lambda offset: later_copy(offset).start())
-
-    def own_copy(offset):
-        other = lax.rem(band + offset, bands)
-        return remote(
-            message, own_in.at[band], own_ss.at[offset], own_rs.at[band], {"lat": other}
-        )
-
-    def own_arrival(offset):
-        other = lax.rem(band + offset, bands)
-        return remote(
-            message, own_in.at[other], own_ss.at[offset], own_rs.at[other], {"lat": other}
-        )
-
-    each(bands, 1, lambda offset: own_copy(offset).start())
-    own_in[band] = share_row
+
+        @pl.when(group > 0)
+        def _():
+            banded(test, field_halo)
+            march(advance_adjoint)
+            add_mapped()
+            fold(((sketch, forced),))
+
+        @pl.when(group == 0)
+        def _():
+            for field in range(fields):
+                ext[field, inside] = combined(test, field)
+                ext[field, before] = jnp.zeros((halo, columns), jnp.float32)
+                ext[field, after] = jnp.zeros((halo, columns), jnp.float32)
+            march(advance_adjoint)
+            add_mapped()
+            for field in range(fields):
+                forced_beyond[field, low] = map_factor * ext[field, before]
+                forced_beyond[field, high] = map_factor * ext[field, after]
+
+            @pl.when(band > 0)
+            def _():
+                beyond_up.wait_recv()
+
+            @pl.when(band < bands - 1)
+            def _():
+                beyond_down.wait_recv()
+
+            fold(((sketch, forced), (beyond, forced_beyond)))
+
+        announce()
 
     each(bands, 1, lambda offset: cost_arrival(offset).wait_recv())
     group_cost = jnp.sum(cost_in[...], axis=0)
@@ -417,27 +529,49 @@
     adjoint_row = jnp.sum(own_in[...], axis=0)
     adjoint[...] = adjoint_row[:, :rank]
     spread_row(adjoint_row)
-    combined(sketch, last_send)
-    marched(advance, last_send, last_recv, last_ss, last_rs)
+
+    @pl.when(group > 0)
+    def _():
+        banded(sketch, last_halo)
+
+    @pl.when(group == 0)
+    def _():
+        for field in range(fields):
+            ext[field, inside] = combined(sketch, field)
+            outer = combined(beyond, field)
+            ext[field, before] = outer[:halo]
+            ext[field, after] = outer[halo:]
+
+    march(advance)
     for field in range(fields):
-        increment[0, field] = ext[field, pl.ds(halo, rows)] / math.sqrt(rank)
+        increment[0, field] = ext[field, inside] / math.sqrt(rank)
 
     each(groups, 1, lambda offset: cost_group_arrival(offset).wait_recv())
     total_cost[...] = jnp.sum(cost_group_in[...], axis=0)[:, :1]
 
-    halo_drain(base_send, base_recv, base_ss, base_rs)
-    halo_drain(last_send, last_recv, last_ss, last_rs)
+    halo_drain(base_halo)
     each(bands, 1, lambda offset: cost_copy(offset).wait_send())
     each(bands, 1, lambda offset: own_copy(offset).wait_send())
     each(groups, 1, lambda offset: cost_group_copy(offset).wait_send())
 
-    @pl.when(group < groups - 1)
-    def _():
-        halo_drain(field_send, field_recv, field_ss, field_rs)
-
     @pl.when(group > 0)
     def _():
+        halo_drain(last_halo)
         each(bands, 0, lambda offset: later_copy(offset).wait_send())
+
+    @pl.when((group > 0) & (group < last_group))
+    def _():
+        halo_drain(field_halo)
+
+    @pl.when(group == 0)
+    def _():
+        @pl.when(band > 0)
+        def _():
+            beyond_down.wait_send()
+
+        @pl.when(band < bands - 1)
+        def _():
+            beyond_up.wait_send()
 
 
 def body(
@@ -455,6 +589,7 @@
     span = rows + 2 * STEPS
     f32 = jnp.float32
     vmem = pl.BlockSpec(memory_space=pltpu.VMEM)
+    hbm = pl.BlockSpec(memory_space=pltpu.HBM)
     edge = pltpu.VMEM((2, fields, STEPS, columns), f32)
     dma = pltpu.SemaphoreType.DMA
     increment, adjoint, cost = pl.pallas_call(
@@ -464,22 +599,20 @@
             jax.ShapeDtypeStruct((1, rank), f32),
             jax.ShapeDtypeStruct((1, 1), f32),
         ),
-        in_specs=[
-            pl.BlockSpec(memory_space=pl.ANY),
-            pl.BlockSpec(memory_space=pl.ANY),
-            vmem,
-            pl.BlockSpec(memory_space=pltpu.SMEM),
-            vmem,
-            vmem,
-            vmem,
-        ],
+        in_specs=[hbm, hbm, hbm, pl.BlockSpec(memory_space=pltpu.SMEM), hbm, hbm, hbm],
         out_specs=(vmem, vmem, vmem),
         scratch_shapes=[
             pltpu.VMEM(sketch.shape, sketch.dtype),
             pltpu.VMEM(test_sketch.shape, test_sketch.dtype),
+            pltpu.VMEM((rank, fields, 2 * STEPS, columns), sketch.dtype),
+            pltpu.VMEM(checkpoints.shape, checkpoints.dtype),
+            pltpu.VMEM(station_row.shape, station_row.dtype),
+            pltpu.VMEM(station_column.shape, station_column.dtype),
+            pltpu.VMEM(station_value.shape, station_value.dtype),
             pltpu.VMEM((fields, span, columns), f32),
             pltpu.VMEM((fields, span, columns), f32),
             pltpu.VMEM((fields, rows, columns), f32),
+            pltpu.VMEM((fields, 2 * STEPS, columns), f32),
             pltpu.VMEM((rank, rows, LANES), f32),
             pltpu.VMEM((rank, LANES), f32),
             edge,
@@ -495,13 +628,15 @@
             pltpu.VMEM((bands, 1, LANES), f32),
             pltpu.VMEM((1, LANES), f32),
             pltpu.VMEM((groups, 1, LANES), f32),
+            dma((6,)),
             dma((2,)),
             dma((2,)),
-            dma((2,)),
-            dma((2,)),
-            dma((2,)),
-            dma((2,)),
-            dma((2,)),
+            dma((2, fields)),
+            dma((2, fields)),
+            dma((2, fields)),
+            dma((2, fields)),
+            dma((2, fields)),
+            dma((2, fields)),
             dma((bands,)),
             dma((bands,)),
             dma((bands,)),
@@ -514,7 +649,7 @@
         compiler_params=pltpu.CompilerParams(
             collective_id=0,
             has_side_effects=True,
-            vmem_limit_bytes=40 * 1024 * 1024,
+            vmem_limit_bytes=67043328,
         ),
     )(
         sketch,

time: 55 us -> 43.4 us (0.79)
  the two profiles are of different devices: /device:TPU:1 before, /device:TPU:0 now
where the time goes in v1:
time: 43.4 us; the launch traced here: 43.2 us
  Pallas kernels  37.5 us (86%)
  between operations  2.97 us (7%)
  local copies, waits for them, and re-layouts  2.73 us (6%)
    pallas_call x1, Pallas kernels, body(): pl.pallas_call(functools.partial(kernel, groups, bands), out_shape=(jax.S...  37.5 us
    unnamed x2, local copies, waits for them, and re-layouts  2.73 us

profile of v1, /device:TPU:0, one launch (start us, length us, event | category | flops | bytes accessed | tf_op | source)
XLA Modules:
  0.0 43.2 jit_solution(2771731683444976548)
XLA Ops:
  1.3 37.5 %shard_map.94 = (f32[1,3,8,1024]{3,2,1,0:T(8,128)}, f32[1,64]{1,0:T(1,128)}, f32[1,1]{1,0:T(1,128)}) custom-call(bf16[64,3,8,1024]{3,2,1,0:T(8,128)(2,1)} %sketch_hbm.1, bf16[64,3,8,1024]{3,2,1,0:T(8,128)(2,1)} %test_hbm.1, bf16[4,3,8,1024]{3,2,1,0:T(8,128)(2,1)} %stored_hbm.1, s32[1]{0:T(128)S(6)} %copy.13.chosen, s32[1,128]{1,0:T(1,128)} %row_hbm.1, ...), custom_call_target="tpu_custom_call" | custom-call | tf_op jit(solution)/shard_map/pallas_call | solution.py:595
  38.8 1.5 %copy.14 = f32[1,3,8,1024]{3,2,1,0:T(8,128)} copy(f32[1,3,8,1024]{3,2,1,0:T(8,128)} %get-tuple-element.12) | data formatting | bytes 196608
  40.3 1.2 %copy.15 = f32[1,64]{1,0:T(1,128)} copy(f32[1,64]{1,0:T(1,128)} %get-tuple-element.13) | data formatting | bytes 512

commit v2 on v1

--- a/solution.py
+++ b/solution.py
@@ -138,24 +138,41 @@
             )
         )
     ]
-    for load in loads:
+    for load in loads[:5]:
         load.start()
 
     barrier = pltpu.get_barrier_semaphore()
-    devices = groups * bands
-    me = group * bands + band
-
-    def greet(offset, carry):
-        other = lax.rem(me + offset, devices)
-        pl.semaphore_signal(
-            barrier,
-            inc=1,
-            device_id={"tm": other // bands, "lat": lax.rem(other, bands)},
-            device_id_type=MESH,
-        )
-        return carry
-
-    lax.fori_loop(1, devices, greet, 0)
+    last_group = groups - 1
+
+    def each(count, first, action):
+        for index in range(first, count):
+            action(index)
+
+    def greet(place):
+        pl.semaphore_signal(barrier, inc=1, device_id=place, device_id_type=MESH)
+
+    @pl.when(group < last_group)
+    def _():
+        each(bands, 0, lambda index: greet({"tm": group + 1, "lat": index}))
+
+    @pl.when(group > 0)
+    def _():
+        each(bands, 0, lambda index: greet({"tm": group - 1, "lat": index}))
+
+    each(bands, 1, lambda offset: greet({"lat": lax.rem(band + offset, bands)}))
+
+    for offset in range(2, groups):
+
+        @pl.when(group + offset < groups)
+        def _():
+            greet({"tm": group + offset})
+
+        @pl.when(group - offset >= 0)
+        def _():
+            greet({"tm": group - offset})
+
+    sides = jnp.minimum(group, 1) + jnp.minimum(last_group - group, 1)
+    greetings = bands - 1 + bands * sides + groups - 1 - sides
 
     def remote(source, target, send_sem, recv_sem, where):
         return pltpu.make_async_remote_copy(
@@ -302,21 +319,17 @@
         share = jnp.sum(jnp.sum(folded[...], axis=1), axis=1, keepdims=True)
         message[...] = jnp.sum(jnp.where(eye, share, 0.0), axis=0, keepdims=True)
 
-    last_group = groups - 1
     loads[4].wait()
 
+    @pl.when(group < last_group)
+    def _():
+        loads[5].start()
+
     @pl.when(group == last_group)
     def _():
         fold(((sketch, forced),))
 
-    pl.semaphore_wait(barrier, devices - 1)
-
-    for field in range(fields):
-        halo_start(base_halo, field)
-
-    def each(count, first, action):
-        for index in range(first, count):
-            action(index)
+    pl.semaphore_wait(barrier, greetings)
 
     def later_copy(offset):
         other = lax.rem(band + offset, bands)
@@ -351,6 +364,9 @@
     @pl.when(group == last_group)
     def _():
         announce()
+
+    for field in range(fields):
+        halo_start(base_halo, field)
 
     def cost_copy(offset):
         other = lax.rem(band + offset, bands)
@@ -451,8 +467,6 @@
         for field in range(fields):
             forced[field] = forced[field] + map_factor * ext[field, inside]
 
-    loads[5].wait()
-
     @pl.when(group < last_group)
     def _():
         def arrive(offset):
@@ -464,6 +478,7 @@
                 {"tm": group, "lat": offset},
             ).wait_recv()
 
+        loads[5].wait()
         each(bands, 0, arrive)
         spread_row(jnp.sum(later_in[...], axis=0))
 
@@ -588,6 +603,10 @@
     rank, fields, rows, columns = sketch.shape
     span = rows + 2 * STEPS
     f32 = jnp.float32
+
+    def in_hbm(array):
+        return pltpu.with_memory_space_constraint(array, pltpu.HBM)
+
     vmem = pl.BlockSpec(memory_space=pltpu.VMEM)
     hbm = pl.BlockSpec(memory_space=pltpu.HBM)
     edge = pltpu.VMEM((2, fields, STEPS, columns), f32)
@@ -649,16 +668,16 @@
         compiler_params=pltpu.CompilerParams(
             collective_id=0,
             has_side_effects=True,
-            vmem_limit_bytes=67043328,
+            vmem_limit_bytes=24 * 1024 * 1024,
         ),
     )(
-        sketch,
-        test_sketch,
-        checkpoints,
+        in_hbm(sketch),
+        in_hbm(test_sketch),
+        in_hbm(checkpoints),
         checkpoint_step,
-        station_row,
-        station_column,
-        station_value,
+        in_hbm(station_row),
+        in_hbm(station_column),
+        in_hbm(station_value),
     )
     return increment, adjoint, cost[0, 0]
 

time: 43.4 us -> 41.1 us (0.947)
  local copies, waits for them, and re-layouts: 2.73 us -> 1.15 us
  Pallas kernels: 37.5 us -> 36.8 us
    unnamed x2, local copies, waits for them, and re-layouts: 2.73 us -> 1.15 us
    pallas_call x1, Pallas kernels: 37.5 us -> 36.8 us  [body(): pl.pallas_call(functools.partial(kernel, groups, bands), out_shape=(jax.S...]
where the time goes in v2:
time: 41.1 us; the launch traced here: 41 us
  Pallas kernels  36.8 us (90%)
  between operations  2.97 us (7%)
  local copies, waits for them, and re-layouts  1.15 us (3%)
    pallas_call x1, Pallas kernels, body(): pl.pallas_call(functools.partial(kernel, groups, bands), out_shape=(jax.S...  36.8 us
    unnamed x2, local copies, waits for them, and re-layouts  1.15 us

profile of v2, /device:TPU:0, one launch (start us, length us, event | category | flops | bytes accessed | tf_op | source)
XLA Modules:
  0.0 41.0 jit_solution(14221362954217357701)
XLA Ops:
  1.3 36.8 %shard_map.94 = (f32[1,3,8,1024]{3,2,1,0:T(8,128)S(1)}, f32[1,64]{1,0:T(1,128)S(1)}, f32[1,1]{1,0:T(1,128)}) custom-call(bf16[64,3,8,1024]{3,2,1,0:T(8,128)(2,1)} %sketch_hbm.1, bf16[64,3,8,1024]{3,2,1,0:T(8,128)(2,1)} %test_hbm.1, bf16[4,3,8,1024]{3,2,1,0:T(8,128)(2,1)} %stored_hbm.1, s32[1]{0:T(128)S(6)} %copy.13.chosen, s32[1,128]{1,0:T(1,128)} %row_hbm.1, ...), custom_call_target="tpu_custom_call" | custom-call | tf_op jit(solution)/shard_map/pallas_call | solution.py:614
  38.1 0.6 %copy.14 = f32[1,3,8,1024]{3,2,1,0:T(8,128)} copy(f32[1,3,8,1024]{3,2,1,0:T(8,128)S(1)} %get-tuple-element.12) | data formatting | bytes 196608
  38.8 0.5 %copy.15 = f32[1,64]{1,0:T(1,128)} copy(f32[1,64]{1,0:T(1,128)S(1)} %get-tuple-element.13) | data formatting | bytes 512
